TPU v7x, 32 devices: a whole 2x2x4 slice. The times are simulated.
32 devices in a mesh: row: 4 (over y, core), col: 8 (over z, x).
Axes of the slice: x: 2, y: 2, z: 4, core: 2. Of those that a mesh axis runs over, the one named last changes fastest.
Arguments:
- excitons: float32 [1024, 1024], P('row', 'col'), may hold values from -500 to 500
- valence_energy: float32 [1024], P('row'), may hold values from -3 to -1
- conduction_energy: float32 [1024], P('col'), may hold values from 1 to 3
- psi_valence: float32 [4096, 1024], P('row', 'col'), may hold values from -0.1875 to 0.1875
- psi_conduction: float32 [4096, 1024], P('col', 'row'), may hold values from -0.1875 to 0.1875
- screened: float32 [4096, 4096], P('row', 'col'), may hold values from -0.9 to 0.975, as said below
Outputs:
- next_vector: float32 [1024, 1024], P('row', 'col')
- coefficients: float32 [4], replicated
Inputs may be any that keep to these rules, and one draw needn't show every extreme that they name: symmetric: screened[p, p'] = screened[p', p].
All inputs are finite; a program needn't handle non-finite values.
Results may differ from a plain program's by a relative error of at most 0.0003.
Values sent between devices are 32-bit elements; how exact they have to be, the bound alone decides.
A program may use at most 64 MiB of HBM per device.

v0:
```python
import jax
import jax.numpy as jnp
from jax import lax
from jax.sharding import PartitionSpec as P

NV = 1024
NC = 1024
STEPS = 2
EPS = 1e-06


def shards(excitons, valence_energy, conduction_energy, psi_valence, psi_conduction, screened):
    high = lax.Precision.HIGHEST
    count = NV * NC
    energy_gap = conduction_energy[None, :] - valence_energy[:, None]
    total = lax.psum(jnp.sum(excitons * excitons), ("row", "col"))
    vector = excitons / jnp.sqrt(total / count + EPS)
    previous = jnp.zeros_like(vector)
    beta_prev = jnp.zeros((), jnp.float32)
    values = []
    for step in range(STEPS):
        panel_valence = lax.all_gather(psi_valence, "col", axis=1, tiled=True)
        panel_conduction = lax.all_gather(psi_conduction, "row", axis=1, tiled=True)
        full_rows = lax.all_gather(vector, "col", axis=1, tiled=True)
        image_block = jnp.dot(full_rows, panel_conduction.T, precision=high)
        image_columns = lax.all_gather(image_block, "row", axis=0, tiled=True)
        points = jnp.dot(panel_valence, image_columns, precision=high)
        weighted = points * screened
        back_valence = lax.psum_scatter(
            jnp.dot(panel_valence.T, weighted, precision=high),
            "row",
            scatter_dimension=0,
            tiled=True,
        )
        back_flipped = back_valence.T
        kernel_flipped = lax.psum_scatter(
            jnp.dot(panel_conduction.T, back_flipped, precision=high),
            "col",
            scatter_dimension=0,
            tiled=True,
        )
        image = energy_gap * vector - kernel_flipped.T
        cross, square, older = lax.psum(
            (jnp.sum(vector * image), jnp.sum(image * image), jnp.sum(previous * image)),
            ("row", "col"),
        )
        alpha = cross / count
        residual = image - alpha * vector - beta_prev * previous
        squared = (
            square / count - alpha * alpha - 2.0 * beta_prev * older / count + beta_prev * beta_prev
        )
        beta = jnp.sqrt(squared + EPS)
        previous = vector
        vector = residual / beta
        beta_prev = beta
        values.append(alpha)
        values.append(beta)
    return (vector, jnp.stack(values))


def solution(mesh):
    return jax.shard_map(
        shards,
        mesh=mesh,
        in_specs=(
            P("row", "col"),
            P("row"),
            P("col"),
            P("row", "col"),
            P("col", "row"),
            P("row", "col"),
        ),
        out_specs=(P("row", "col"), P()),
        check_vma=False,
    )
```

profile of v0, /device:TPU:0, one launch (start us, length us, event | category | flops | bytes accessed | tf_op | source)
XLA Modules:
  0.0 619.4 jit_solution(2300817398218281370)
XLA Ops:
  7.2 1.5 multiply_reduce_fusion.6
  8.8 42.2 %psum.49 = f32[]{:T(128)} all-reduce(f32[]{:T(128)} %multiply_reduce_fusion.6), channel_id=1, replica_groups=mesh['row'=4,'col'=8] {'row','col'}, use_global_device_ids=true, to_apply=%region_1.0 | all-reduce | flops 1 | bytes 8 | tf_op jit(solution)/shard_map/psum | solution.py:16
  51.6 1.6 broadcast_divide_fusion
  53.3 0.7 all-gather.9.cloned.1.call-update
  54.0 38.7 %all-gather.7.cloned.1.call-done = f32[256,1024]{1,0:T(8,128)} async-done(((f32[256,128]{1,0:T(8,128)}), f32[256,1024]{1,0:T(8,128)}) %all-gather.7.cloned.1.call-update) | async-done | bytes 1048592 | tf_op jit(solution)/shard_map/all_gather | solution.py:24
  92.8 23.2 %all-gather.9.cloned.1.call-done = f32[512,1024]{1,0:T(8,128)} async-done(((f32[512,256]{1,0:T(8,128)}), f32[512,1024]{1,0:T(8,128)}) %all-gather.9.cloned.1.call-update) | async-done | bytes 2097168 | tf_op jit(solution)/shard_map/all_gather | solution.py:23
  115.9 4.7 fusion.6
  120.7 0.5 all-gather.13.cloned.1.call-update
  121.5 21.9 %all-gather.11.cloned.1.call-done = f32[1024,512]{1,0:T(8,128)} async-done(((f32[256,512]{1,0:T(8,128)}), f32[1024,512]{1,0:T(8,128)}) %all-gather.11.cloned.1.call-update) | async-done | bytes 2097168 | tf_op jit(solution)/shard_map/all_gather | solution.py:26
  143.4 76.6 %all-gather.13.cloned.1.call-done = f32[1024,1024]{1,0:T(8,128)} async-done(((f32[1024,128]{1,0:T(8,128)}), f32[1024,1024]{1,0:T(8,128)}) %all-gather.13.cloned.1.call-update) | async-done | bytes 4194320 | tf_op jit(solution)/shard_map/all_gather | solution.py:22
  219.9 9.4 %fusion.7 = f32[512,1024]{0,1:T(8,128)S(1)} fusion(f32[1024,512]{1,0:T(8,128)} %all-gather.11.cloned.1.call-done, f32[1024,1024]{1,0:T(8,128)} %all-gather.13.cloned.1.call-done), kind=kOutput, calls=%fused_computation.24 | convolution fusion | flops 6442450944 | bytes 8388608 | tf_op jit(solution)/shard_map/dot_general | solution.py:27
  229.4 8.2 %fusion.2 = f32[1024,512]{0,1:T(8,128)} fusion(f32[1024,1024]{1,0:T(8,128)S(1)} %copy-done, f32[1024,512]{1,0:T(8,128)S(1)} %copy-done.3, f32[512,1024]{0,1:T(8,128)S(1)} %fusion.7), kind=kOutput, calls=%fused_computation.4 | convolution fusion | flops 6442975232 | bytes 10485760 | tf_op jit(solution)/shard_map/dot_general | solution.py:30
  237.7 0.3 reduce-scatter.7.cloned.1.call-start
  238.0 29.2 %reduce-scatter.5.cloned.1.call-done = f32[256,512]{0,1:T(8,128)} async-done(((f32[1024,512]{0,1:T(8,128)}), f32[256,512]{0,1:T(8,128)}) %reduce-scatter.5.cloned.1.call-update) | async-done | bytes 524304 | tf_op jit(solution)/shard_map/reduce_scatter | solution.py:29
  267.2 3.9 convolution_bitcast_fusion.1
  271.1 64.8 %reduce-scatter.7.cloned.1.call-done = f32[128,256]{0,1:T(8,128)} async-done(((f32[1024,256]{0,1:T(8,128)}), f32[128,256]{0,1:T(8,128)}) %reduce-scatter.7.cloned.1.call-update) | async-done | bytes 131088 | tf_op jit(solution)/shard_map/reduce_scatter | solution.py:36
  335.9 1.6 multiply_reduce_fusion.3
  337.5 40.1 %all-reduce.1 = (f32[]{:T(128)}, f32[]{:T(128)}, f32[]{:T(128)}) all-reduce(f32[]{:T(128)} %get-tuple-element.6, f32[]{:T(128)} %get-tuple-element.7, f32[]{:T(128)} %get-tuple-element.5), channel_id=1, replica_groups=mesh['row'=4,'col'=8] {'row','col'}, use_global_device_ids=true, to_apply=%region_7.0 | all-reduce | flops 3 | bytes 24 | tf_op jit(solution)/shard_map/psum | solution.py:43
  381.1 1.7 subtract_divide_fusion.1
  382.8 38.9 %all-gather.15.cloned.1.call-done = f32[256,1024]{1,0:T(8,128)} async-done(((f32[256,128]{1,0:T(8,128)}), f32[256,1024]{1,0:T(8,128)}) %all-gather.15.cloned.1.call-update) | async-done | bytes 1048592 | tf_op jit(solution)/shard_map/all_gather | solution.py:24
  421.7 4.0 fusion.8
  425.8 21.7 %all-gather.17.cloned.1.call-done = f32[1024,512]{1,0:T(8,128)} async-done(((f32[256,512]{1,0:T(8,128)}), f32[1024,512]{1,0:T(8,128)}) %all-gather.17.cloned.1.call-update) | async-done | bytes 2097168 | tf_op jit(solution)/shard_map/all_gather | solution.py:26
  447.5 9.4 %fusion.9 = f32[512,1024]{0,1:T(8,128)S(1)} fusion(f32[1024,512]{1,0:T(8,128)} %all-gather.17.cloned.1.call-done, f32[1024,1024]{1,0:T(8,128)} %all-gather.13.cloned.1.call-done), kind=kOutput, calls=%fused_computation.26 | convolution fusion | flops 6442450944 | bytes 8388608 | tf_op jit(solution)/shard_map/dot_general | solution.py:27
  456.9 8.2 %fusion.3 = f32[1024,512]{0,1:T(8,128)} fusion(f32[1024,1024]{1,0:T(8,128)S(1)} %copy-done.1, f32[1024,512]{1,0:T(8,128)S(1)} %copy-done.4, f32[512,1024]{0,1:T(8,128)S(1)} %fusion.9), kind=kOutput, calls=%fused_computation.5 | convolution fusion | flops 6442975232 | bytes 10485760 | tf_op jit(solution)/shard_map/dot_general | solution.py:30
  465.2 0.3 reduce-scatter.11.cloned.1.call-start
  465.5 31.0 %reduce-scatter.9.cloned.1.call-done = f32[256,512]{0,1:T(8,128)} async-done(((f32[1024,512]{0,1:T(8,128)}), f32[256,512]{0,1:T(8,128)}) %reduce-scatter.9.cloned.1.call-update) | async-done | bytes 524304 | tf_op jit(solution)/shard_map/reduce_scatter | solution.py:29
  496.5 3.9 convolution_bitcast_fusion
  500.4 64.8 %reduce-scatter.11.cloned.1.call-done = f32[128,256]{0,1:T(8,128)} async-done(((f32[1024,256]{0,1:T(8,128)}), f32[128,256]{0,1:T(8,128)}) %reduce-scatter.11.cloned.1.call-update) | async-done | bytes 131088 | tf_op jit(solution)/shard_map/reduce_scatter | solution.py:36
  565.3 1.7 multiply_reduce_fusion
  566.9 40.1 %all-reduce = (f32[]{:T(128)}, f32[]{:T(128)}, f32[]{:T(128)}) all-reduce(f32[]{:T(128)} %get-tuple-element.3, f32[]{:T(128)} %get-tuple-element.4, f32[]{:T(128)} %get-tuple-element.2), channel_id=1, replica_groups=mesh['row'=4,'col'=8] {'row','col'}, use_global_device_ids=true, to_apply=%region_15.0 | all-reduce | flops 3 | bytes 24 | tf_op jit(solution)/shard_map/psum | solution.py:43
  610.3 0.6 pad_maximum_fusion
  610.9 1.7 subtract_divide_fusion
  (34 shorter events, 0.7 us)
Async XLA Ops:
  7.2 85.6 %all-gather.7.cloned.1.call-start = ((), (), s32[]{:S(2)}) async-start(), calls=%async_computation.4 | async-start | bytes 1179648 | tf_op jit(solution)/shard_map/all_gather | solution.py:24
  53.2 62.7 %all-gather.9.cloned.1.call-start = ((), (), s32[]{:S(2)}) async-start(), calls=%async_computation.5 | async-start | bytes 2621440 | tf_op jit(solution)/shard_map/all_gather | solution.py:23
  54.0 89.4 %all-gather.11.cloned.1.call-start = ((), (), s32[]{:S(2)}) async-start(), calls=%async_computation.6 | async-start | bytes 2621440 | tf_op jit(solution)/shard_map/all_gather | solution.py:26
  120.7 99.3 %all-gather.13.cloned.1.call-start = ((), (), s32[]{:S(2)}) async-start(), calls=%async_computation.7 | async-start | bytes 4718592 | tf_op jit(solution)/shard_map/all_gather | solution.py:22
  121.2 108.1 %copy-start.3 = (f32[1024,512]{1,0:T(8,128)S(1)}, f32[1024,512]{1,0:T(8,128)}, u32[]{:S(2)}) copy-start(f32[1024,512]{1,0:T(8,128)} %param.11) | copy-start | bytes 6291460
  121.3 145.9 %reduce-scatter.5.cloned.1.call-start = ((), (), s32[]{:S(2)}) async-start(), calls=%async_computation.8 | async-start | bytes 2621440 | tf_op jit(solution)/shard_map/reduce_scatter | solution.py:29
  219.9 9.4 %copy-start = (f32[1024,1024]{1,0:T(8,128)S(1)}, f32[1024,1024]{1,0:T(8,128)}, u32[]{:S(2)}) copy-start(f32[1024,1024]{1,0:T(8,128)} %all-gather.13.cloned.1.call-done) | copy-start | bytes 12582916
  237.7 29.5 %copy-start.2 = (f32[512,1024]{1,0:T(8,128)S(1)}, f32[512,1024]{1,0:T(8,128)}, u32[]{:S(2)}) copy-start(f32[512,1024]{1,0:T(8,128)} %all-gather.9.cloned.1.call-done) | copy-start | bytes 6291460
  237.7 98.2 %copy-start.5 = (f32[256,128]{1,0:T(8,128)S(1)}, f32[256,128]{1,0:T(8,128)}, u32[]{:S(2)}) copy-start(f32[256,128]{1,0:T(8,128)} %param.6) | copy-start | bytes 393220
  237.7 98.2 %copy-start.7 = (f32[256]{0:T(256)S(1)}, f32[256]{0:T(256)}, u32[]{:S(2)}) copy-start(f32[256]{0:T(256)} %param.7) | copy-start | bytes 3076
  237.7 98.2 %copy-start.8 = (f32[128]{0:T(128)S(1)}, f32[128]{0:T(128)}, u32[]{:S(2)}) copy-start(f32[128]{0:T(128)} %param.8) | copy-start | bytes 1540
  237.7 98.2 %reduce-scatter.7.cloned.1.call-start = ((), (), s32[]{:S(2)}) async-start(), calls=%async_computation.9 | async-start | bytes 1179648 | tf_op jit(solution)/shard_map/reduce_scatter | solution.py:36
  271.1 150.6 %all-gather.15.cloned.1.call-start = ((), (), s32[]{:S(2)}) async-start(), calls=%async_computation.10 | async-start | bytes 1179648 | tf_op jit(solution)/shard_map/all_gather | solution.py:24
  382.8 64.7 %all-gather.17.cloned.1.call-start = ((), (), s32[]{:S(2)}) async-start(), calls=%async_computation.11 | async-start | bytes 2621440 | tf_op jit(solution)/shard_map/all_gather | solution.py:26
  425.7 70.8 %reduce-scatter.9.cloned.1.call-start = ((), (), s32[]{:S(2)}) async-start(), calls=%async_computation.12 | async-start | bytes 2621440 | tf_op jit(solution)/shard_map/reduce_scatter | solution.py:29
  447.4 9.4 %copy-start.1 = (f32[1024,1024]{1,0:T(8,128)S(1)}, f32[1024,1024]{1,0:T(8,128)}, u32[]{:S(2)}) copy-start(f32[1024,1024]{1,0:T(8,128)} %all-gather.13.cloned.1.call-done) | copy-start | bytes 12582916
  447.5 9.4 %copy-start.4 = (f32[1024,512]{1,0:T(8,128)S(1)}, f32[1024,512]{1,0:T(8,128)}, u32[]{:S(2)}) copy-start(f32[1024,512]{1,0:T(8,128)} %param.11) | copy-start | bytes 6291460
  465.2 100.1 %copy-start.6 = (f32[256,128]{1,0:T(8,128)S(1)}, f32[256,128]{1,0:T(8,128)}, u32[]{:S(2)}) copy-start(f32[256,128]{1,0:T(8,128)} %subtract_divide_fusion.1) | copy-start | bytes 393220
  465.2 100.1 %reduce-scatter.11.cloned.1.call-start = ((), (), s32[]{:S(2)}) async-start(), calls=%async_computation.13 | async-start | bytes 1179648 | tf_op jit(solution)/shard_map/reduce_scatter | solution.py:36
Sparse Core Ops, SparseCore 0:
  53.3 39.3 all-gather.6
  94.3 21.5 all-gather.8
  120.8 22.5 all-gather.10
  145.3 74.6 all-gather.12
  237.8 29.3 reduce-scatter.4
  271.2 64.6 reduce-scatter.6
  382.9 38.7 all-gather.14
  425.8 21.5 all-gather.16
  465.3 31.1 reduce-scatter.8
  500.5 64.6 reduce-scatter.10
where the time goes:
time: 620 us; the launch traced here: 619 us
  waiting for transfers between devices  412 us (66%)
  blocking collectives  122 us (20%)
  matrix products  51.8 us (8%)
  between operations  21.6 us (3%)
  other arithmetic  10.3 us (2%)
    reduce_scatter x2, waiting for transfers between devices, shards(): lax.psum_scatter(jnp.dot(panel_conduction.T, back_flipped, precision=high...  130 us
    psum x2, blocking collectives, shards(): lax.psum((jnp.sum(vector * image), jnp.sum(image * image), jnp.sum(previo...  80.3 us
    all_gather x2, waiting for transfers between devices, shards(): full_rows = lax.all_gather(vector, 'col', axis=1, tiled=True)  77.6 us
    all_gather x1, waiting for transfers between devices, shards(): panel_valence = lax.all_gather(psi_valence, 'col', axis=1, tiled=True)  76.6 us
    reduce_scatter x2, waiting for transfers between devices, shards(): lax.psum_scatter(jnp.dot(panel_valence.T, weighted, precision=high), 'row...  60.2 us
    all_gather x2, waiting for transfers between devices, shards(): image_columns = lax.all_gather(image_block, 'row', axis=0, tiled=True)  43.6 us
    psum x1, blocking collectives, shards(): total = lax.psum(jnp.sum(excitons * excitons), ('row', 'col'))  42.2 us
    all_gather x1, waiting for transfers between devices, shards(): panel_conduction = lax.all_gather(psi_conduction, 'row', axis=1, tiled=True)  23.2 us
  transfers between devices with their start and end apart: 10, of which 10 were waited for; matrix products, arithmetic and copies ran while one was open for 0% of the time, Pallas kernels for 0%

commit v1 on v0

--- a/solution.py
+++ b/solution.py
@@ -23,7 +23,14 @@
         panel_conduction = lax.all_gather(psi_conduction, "row", axis=1, tiled=True)
         full_rows = lax.all_gather(vector, "col", axis=1, tiled=True)
         image_block = jnp.dot(full_rows, panel_conduction.T, precision=high)
-        image_columns = lax.all_gather(image_block, "row", axis=0, tiled=True)
+        ring = [image_block]
+        for hop in range(3):
+            ring.append(lax.ppermute(ring[-1], "row", [(dev, (dev + 1) % 4) for dev in range(4)]))
+        image_columns = jnp.roll(
+            jnp.concatenate(ring[::-1], axis=0),
+            (lax.axis_index("row") + 1) * ring[0].shape[0],
+            axis=0,
+        )
         points = jnp.dot(panel_valence, image_columns, precision=high)
         weighted = points * screened
         back_valence = lax.psum_scatter(

time: 620 us -> 600 us (0.968)
  waiting for transfers between devices: 412 us -> 389 us
    ppermute x0 -> x6, waiting for transfers between devices: none -> 51.8 us  [shards(): lax.ppermute(ring[-1], 'row', [(dev, (dev + 1) % 4) for dev in range(4)])]
    all_gather x2 -> x0, waiting for transfers between devices: 43.6 us -> none  [shards(): image_columns = lax.all_gather(image_block, 'row', axis=0, tiled=True)]
    all_gather x1, waiting for transfers between devices: 76.6 us -> 46.6 us  [shards(): panel_valence = lax.all_gather(psi_valence, 'col', axis=1, tiled=True)]
  transfers between devices with their start and end apart: 10 -> 14, of which waited for: 10 -> 14; matrix products, arithmetic and copies ran while one was open for 0% -> 1% of each run, Pallas kernels for 0% -> 0%
where the time goes in v1:
time: 600 us; the launch traced here: 599 us
  waiting for transfers between devices  389 us (65%)
  blocking collectives  122 us (20%)
  matrix products  54.4 us (9%)
  between operations  21.6 us (4%)
  other arithmetic  10.3 us (2%)
    reduce_scatter x2, waiting for transfers between devices, shards(): lax.psum_scatter(jnp.dot(panel_conduction.T, back_flipped, precision=high...  130 us
    psum x2, blocking collectives, shards(): lax.psum((jnp.sum(vector * image), jnp.sum(image * image), jnp.sum(previo...  80.2 us
    all_gather x2, waiting for transfers between devices, shards(): full_rows = lax.all_gather(vector, 'col', axis=1, tiled=True)  76.8 us
    reduce_scatter x2, waiting for transfers between devices, shards(): lax.psum_scatter(jnp.dot(panel_valence.T, weighted, precision=high), 'row...  59.2 us
    ppermute x6, waiting for transfers between devices, shards(): lax.ppermute(ring[-1], 'row', [(dev, (dev + 1) % 4) for dev in range(4)])  51.8 us
    all_gather x1, waiting for transfers between devices, shards(): panel_valence = lax.all_gather(psi_valence, 'col', axis=1, tiled=True)  46.6 us
    psum x1, blocking collectives, shards(): total = lax.psum(jnp.sum(excitons * excitons), ('row', 'col'))  42.2 us
    all_gather x1, waiting for transfers between devices, shards(): panel_conduction = lax.all_gather(psi_conduction, 'row', axis=1, tiled=True)  23.2 us
  transfers between devices with their start and end apart: 14, of which 14 were waited for; matrix products, arithmetic and copies ran while one was open for 1% of the time, Pallas kernels for 0%

profile of v1, /device:TPU:0, one launch (start us, length us, event | category | flops | bytes accessed | tf_op | source)
XLA Modules:
  0.0 598.8 jit_solution(1957625028516633071)
XLA Ops:
  7.2 1.5 multiply_reduce_fusion.6
  8.8 42.2 %psum.49 = f32[]{:T(128)} all-reduce(f32[]{:T(128)} %multiply_reduce_fusion.6), channel_id=1, replica_groups=mesh['row'=4,'col'=8] {'row','col'}, use_global_device_ids=true, to_apply=%region_1.0 | all-reduce | flops 1 | bytes 8 | tf_op jit(solution)/shard_map/psum | solution.py:16
  51.6 1.6 broadcast_divide_fusion
  53.3 0.7 all-gather.7.cloned.1.call-update
  54.8 38.0 %all-gather.5.cloned.1.call-done = f32[256,1024]{1,0:T(8,128)} async-done(((f32[256,128]{1,0:T(8,128)}), f32[256,1024]{1,0:T(8,128)}) %all-gather.5.cloned.1.call-update) | async-done | bytes 1048592 | tf_op jit(solution)/shard_map/all_gather | solution.py:24
  92.8 23.2 %all-gather.7.cloned.1.call-done = f32[512,1024]{1,0:T(8,128)} async-done(((f32[512,256]{1,0:T(8,128)}), f32[512,1024]{1,0:T(8,128)}) %all-gather.7.cloned.1.call-update) | async-done | bytes 2097168 | tf_op jit(solution)/shard_map/all_gather | solution.py:23
  115.9 3.9 fusion.30
  120.1 8.4 %collective-permute-done = f32[256,512]{1,0:T(8,128)S(1)} collective-permute-done((f32[256,512]{1,0:T(8,128)S(1)}, f32[256,512]{1,0:T(8,128)S(1)}, u32[]{:S(2)}, u32[]{:S(2)}) %collective-permute-start) | collective-permute-done | bytes 524320 | tf_op jit(solution)/shard_map/ppermute | solution.py:28
  128.5 8.7 %collective-permute-done.1 = f32[256,512]{1,0:T(8,128)} collective-permute-done((f32[256,512]{1,0:T(8,128)S(1)}, f32[256,512]{1,0:T(8,128)}, u32[]{:S(2)}, u32[]{:S(2)}) %collective-permute-start.1) | collective-permute-done | bytes 524320 | tf_op jit(solution)/shard_map/ppermute | solution.py:28
  137.2 8.9 %collective-permute-done.2 = f32[256,512]{1,0:T(8,128)} collective-permute-done((f32[256,512]{1,0:T(8,128)}, f32[256,512]{1,0:T(8,128)}, u32[]{:S(2)}, u32[]{:S(2)}) %collective-permute-start.2) | collective-permute-done | bytes 524320 | tf_op jit(solution)/shard_map/ppermute | solution.py:28
  146.1 46.6 %all-gather.9.cloned.1.call-done = f32[1024,1024]{1,0:T(8,128)} async-done(((f32[1024,128]{1,0:T(8,128)}), f32[1024,1024]{1,0:T(8,128)}) %all-gather.9.cloned.1.call-update) | async-done | bytes 4194320 | tf_op jit(solution)/shard_map/all_gather | solution.py:22
  192.6 11.2 %fusion.14 = f32[512,1024]{0,1:T(8,128)S(1)} fusion(f32[1024,1024]{1,0:T(8,128)} %all-gather.9.cloned.1.call-done, s32[]{:T(128)S(6)} %select_n.13, f32[256,512]{1,0:T(8,128)} %collective-permute-done.2, f32[256,512]{1,0:T(8,128)} %collective-permute-done.1, f32[256,512]{1,0:T(8,128)S(1)} %collective-permute-done, f32[256,512]{1,0:T(8,128)S(1)} %fusion.30), kind=kOutput, calls=%fused_computation.28 | convolution fusion | flops 6446120960 | bytes 8388612 | tf_op jit(solution)/shard_map/dot_general | solution.py:34
  203.9 8.3 %fusion.22 = f32[1024,512]{0,1:T(8,128)} fusion(f32[1024,1024]{1,0:T(8,128)S(1)} %copy-done.1, f32[1024,512]{1,0:T(8,128)S(1)} %copy-done.3, f32[512,1024]{0,1:T(8,128)S(1)} %fusion.14), kind=kOutput, calls=%fused_computation.36 | convolution fusion | flops 6442975232 | bytes 10485760 | tf_op jit(solution)/shard_map/dot_general | solution.py:37
  212.5 29.2 %reduce-scatter.5.cloned.1.call-done = f32[256,512]{0,1:T(8,128)} async-done(((f32[1024,512]{0,1:T(8,128)}), f32[256,512]{0,1:T(8,128)}) %reduce-scatter.5.cloned.1.call-update) | async-done | bytes 524304 | tf_op jit(solution)/shard_map/reduce_scatter | solution.py:36
  241.6 3.9 convolution_bitcast_fusion.1
  245.6 65.0 %reduce-scatter.7.cloned.1.call-done = f32[128,256]{0,1:T(8,128)} async-done(((f32[1024,256]{0,1:T(8,128)}), f32[128,256]{0,1:T(8,128)}) %reduce-scatter.7.cloned.1.call-update) | async-done | bytes 131088 | tf_op jit(solution)/shard_map/reduce_scatter | solution.py:43
  310.6 1.6 multiply_reduce_fusion.3
  312.2 40.1 %all-reduce.1 = (f32[]{:T(128)}, f32[]{:T(128)}, f32[]{:T(128)}) all-reduce(f32[]{:T(128)} %get-tuple-element.7, f32[]{:T(128)} %get-tuple-element.8, f32[]{:T(128)} %get-tuple-element.6), channel_id=1, replica_groups=mesh['row'=4,'col'=8] {'row','col'}, use_global_device_ids=true, to_apply=%region_7.9 | all-reduce | flops 3 | bytes 24 | tf_op jit(solution)/shard_map/psum | solution.py:50
  355.8 1.7 subtract_divide_fusion.1
  357.5 38.8 %all-gather.11.cloned.1.call-done = f32[256,1024]{1,0:T(8,128)} async-done(((f32[256,128]{1,0:T(8,128)}), f32[256,1024]{1,0:T(8,128)}) %all-gather.11.cloned.1.call-update) | async-done | bytes 1048592 | tf_op jit(solution)/shard_map/all_gather | solution.py:24
  396.4 3.2 fusion.31
  399.6 8.6 %collective-permute-done.3 = f32[256,512]{1,0:T(8,128)S(1)} collective-permute-done((f32[256,512]{1,0:T(8,128)S(1)}, f32[256,512]{1,0:T(8,128)S(1)}, u32[]{:S(2)}, u32[]{:S(2)}) %collective-permute-start.3) | collective-permute-done | bytes 524320 | tf_op jit(solution)/shard_map/ppermute | solution.py:28
  408.2 8.6 %collective-permute-done.4 = f32[256,512]{1,0:T(8,128)S(1)} collective-permute-done((f32[256,512]{1,0:T(8,128)S(1)}, f32[256,512]{1,0:T(8,128)S(1)}, u32[]{:S(2)}, u32[]{:S(2)}) %collective-permute-start.4) | collective-permute-done | bytes 524320 | tf_op jit(solution)/shard_map/ppermute | solution.py:28
  416.8 8.6 %collective-permute-done.5 = f32[256,512]{1,0:T(8,128)S(1)} collective-permute-done((f32[256,512]{1,0:T(8,128)S(1)}, f32[256,512]{1,0:T(8,128)S(1)}, u32[]{:S(2)}, u32[]{:S(2)}) %collective-permute-start.5) | collective-permute-done | bytes 524320 | tf_op jit(solution)/shard_map/ppermute | solution.py:28
  425.4 11.9 %fusion.4 = f32[512,1024]{0,1:T(8,128)S(1)} fusion(f32[1024,1024]{1,0:T(8,128)} %all-gather.9.cloned.1.call-done, s32[]{:T(128)S(6)} %select_n.13, f32[256,512]{1,0:T(8,128)S(1)} %collective-permute-done.5, f32[256,512]{1,0:T(8,128)S(1)} %collective-permute-done.4, f32[256,512]{1,0:T(8,128)S(1)} %collective-permute-done.3, f32[256,512]{1,0:T(8,128)S(1)} %fusion.31), kind=kOutput, calls=%fused_computation.20 | convolution fusion | flops 6446120960 | bytes 8388612 | tf_op jit(solution)/shard_map/dot_general | solution.py:34
  437.3 8.3 %fusion.23 = f32[1024,512]{0,1:T(8,128)} fusion(f32[1024,1024]{1,0:T(8,128)S(1)} %copy-done.2, f32[1024,512]{1,0:T(8,128)S(1)} %copy-done.4, f32[512,1024]{0,1:T(8,128)S(1)} %fusion.4), kind=kOutput, calls=%fused_computation.37 | convolution fusion | flops 6442975232 | bytes 10485760 | tf_op jit(solution)/shard_map/dot_general | solution.py:37
  446.0 30.0 %reduce-scatter.9.cloned.1.call-done = f32[256,512]{0,1:T(8,128)} async-done(((f32[1024,512]{0,1:T(8,128)}), f32[256,512]{0,1:T(8,128)}) %reduce-scatter.9.cloned.1.call-update) | async-done | bytes 524304 | tf_op jit(solution)/shard_map/reduce_scatter | solution.py:36
  476.0 3.9 convolution_bitcast_fusion
  479.9 64.8 %reduce-scatter.11.cloned.1.call-done = f32[128,256]{0,1:T(8,128)} async-done(((f32[1024,256]{0,1:T(8,128)}), f32[128,256]{0,1:T(8,128)}) %reduce-scatter.11.cloned.1.call-update) | async-done | bytes 131088 | tf_op jit(solution)/shard_map/reduce_scatter | solution.py:43
  544.7 1.7 multiply_reduce_fusion
  546.4 40.1 %all-reduce = (f32[]{:T(128)}, f32[]{:T(128)}, f32[]{:T(128)}) all-reduce(f32[]{:T(128)} %get-tuple-element.4, f32[]{:T(128)} %get-tuple-element.5, f32[]{:T(128)} %get-tuple-element.3), channel_id=1, replica_groups=mesh['row'=4,'col'=8] {'row','col'}, use_global_device_ids=true, to_apply=%region_15.17 | all-reduce | flops 3 | bytes 24 | tf_op jit(solution)/shard_map/psum | solution.py:50
  590.3 1.7 subtract_divide_fusion
  (40 shorter events, 2.6 us)
Async XLA Ops:
  7.2 85.6 %all-gather.5.cloned.1.call-start = ((), (), s32[]{:S(2)}) async-start(), calls=%async_computation.4 | async-start | bytes 1179648 | tf_op jit(solution)/shard_map/all_gather | solution.py:24
  53.2 62.7 %all-gather.7.cloned.1.call-start = ((), (), s32[]{:S(2)}) async-start(), calls=%async_computation.5 | async-start | bytes 2621440 | tf_op jit(solution)/shard_map/all_gather | solution.py:23
  54.0 138.7 %all-gather.9.cloned.1.call-start = ((), (), s32[]{:S(2)}) async-start(), calls=%async_computation.6 | async-start | bytes 4718592 | tf_op jit(solution)/shard_map/all_gather | solution.py:22
  54.7 186.9 %reduce-scatter.5.cloned.1.call-start = ((), (), s32[]{:S(2)}) async-start(), calls=%async_computation.7 | async-start | bytes 2621440 | tf_op jit(solution)/shard_map/reduce_scatter | solution.py:36
  119.8 8.7 %collective-permute-start = (f32[256,512]{1,0:T(8,128)S(1)}, f32[256,512]{1,0:T(8,128)S(1)}, u32[]{:S(2)}, u32[]{:S(2)}) collective-permute-start(f32[256,512]{1,0:T(8,128)S(1)} %fusion.30), channel_id=1, source_target_pairs={{0,8},{8,16},{16,24},{24,0},{1,9},{9,17},{17,25},{25,1},{2,10},{10... | collective-permute-start | bytes 1572872 | tf_op jit(solution)/shard_map/ppermute | solution.py:28
  128.5 8.7 %collective-permute-start.1 = (f32[256,512]{1,0:T(8,128)S(1)}, f32[256,512]{1,0:T(8,128)}, u32[]{:S(2)}, u32[]{:S(2)}) collective-permute-start(f32[256,512]{1,0:T(8,128)S(1)} %collective-permute-done), channel_id=1, source_target_pairs={{0,8},{8,16},{16,24},{24,0},{1,9},{9,17},{17,25},{25,1},{2,10},{10... | collective-permute-start | bytes 1572872 | tf_op jit(solution)/shard_map/ppermute | solution.py:28
  137.2 8.9 %collective-permute-start.2 = (f32[256,512]{1,0:T(8,128)}, f32[256,512]{1,0:T(8,128)}, u32[]{:S(2)}, u32[]{:S(2)}) collective-permute-start(f32[256,512]{1,0:T(8,128)} %collective-permute-done.1), channel_id=1, source_target_pairs={{0,8},{8,16},{16,24},{24,0},{1,9},{9,17},{17,25},{25,1},{2,10},{10... | collective-permute-start | bytes 1572872 | tf_op jit(solution)/shard_map/ppermute | solution.py:28
  137.2 66.7 %copy-start.3 = (f32[1024,512]{1,0:T(8,128)S(1)}, f32[1024,512]{1,0:T(8,128)}, u32[]{:S(2)}) copy-start(f32[1024,512]{1,0:T(8,128)} %param.13) | copy-start | bytes 6291460
  192.6 11.2 %copy-start.1 = (f32[1024,1024]{1,0:T(8,128)S(1)}, f32[1024,1024]{1,0:T(8,128)}, u32[]{:S(2)}) copy-start(f32[1024,1024]{1,0:T(8,128)} %all-gather.9.cloned.1.call-done) | copy-start | bytes 12582916
  212.1 29.5 %copy-start = (f32[512,1024]{1,0:T(8,128)S(1)}, f32[512,1024]{1,0:T(8,128)}, u32[]{:S(2)}) copy-start(f32[512,1024]{1,0:T(8,128)} %all-gather.7.cloned.1.call-done) | copy-start | bytes 6291460
  212.2 98.5 %copy-start.5 = (f32[256,128]{1,0:T(8,128)S(1)}, f32[256,128]{1,0:T(8,128)}, u32[]{:S(2)}) copy-start(f32[256,128]{1,0:T(8,128)} %param.8) | copy-start | bytes 393220
  212.2 98.4 %copy-start.7 = (f32[256]{0:T(256)S(1)}, f32[256]{0:T(256)}, u32[]{:S(2)}) copy-start(f32[256]{0:T(256)} %param.9) | copy-start | bytes 3076
  212.2 98.4 %copy-start.8 = (f32[128]{0:T(128)S(1)}, f32[128]{0:T(128)}, u32[]{:S(2)}) copy-start(f32[128]{0:T(128)} %param.10) | copy-start | bytes 1540
  212.2 98.4 %reduce-scatter.7.cloned.1.call-start = ((), (), s32[]{:S(2)}) async-start(), calls=%async_computation.8 | async-start | bytes 1179648 | tf_op jit(solution)/shard_map/reduce_scatter | solution.py:43
  245.5 150.8 %all-gather.11.cloned.1.call-start = ((), (), s32[]{:S(2)}) async-start(), calls=%async_computation.9 | async-start | bytes 1179648 | tf_op jit(solution)/shard_map/all_gather | solution.py:24
  357.5 118.5 %reduce-scatter.9.cloned.1.call-start = ((), (), s32[]{:S(2)}) async-start(), calls=%async_computation.10 | async-start | bytes 2621440 | tf_op jit(solution)/shard_map/reduce_scatter | solution.py:36
  399.5 37.8 %copy-start.4 = (f32[1024,512]{1,0:T(8,128)S(1)}, f32[1024,512]{1,0:T(8,128)}, u32[]{:S(2)}) copy-start(f32[1024,512]{1,0:T(8,128)} %param.13) | copy-start | bytes 6291460
  399.6 8.7 %collective-permute-start.3 = (f32[256,512]{1,0:T(8,128)S(1)}, f32[256,512]{1,0:T(8,128)S(1)}, u32[]{:S(2)}, u32[]{:S(2)}) collective-permute-start(f32[256,512]{1,0:T(8,128)S(1)} %fusion.31), channel_id=1, source_target_pairs={{0,8},{8,16},{16,24},{24,0},{1,9},{9,17},{17,25},{25,1},{2,10},{10... | collective-permute-start | bytes 1572872 | tf_op jit(solution)/shard_map/ppermute | solution.py:28
  408.2 8.6 %collective-permute-start.4 = (f32[256,512]{1,0:T(8,128)S(1)}, f32[256,512]{1,0:T(8,128)S(1)}, u32[]{:S(2)}, u32[]{:S(2)}) collective-permute-start(f32[256,512]{1,0:T(8,128)S(1)} %collective-permute-done.3), channel_id=1, source_target_pairs={{0,8},{8,16},{16,24},{24,0},{1,9},{9,17},{17,25},{25,1},{2,10},{10... | collective-permute-start | bytes 1572872 | tf_op jit(solution)/shard_map/ppermute | solution.py:28
  416.8 8.6 %collective-permute-start.5 = (f32[256,512]{1,0:T(8,128)S(1)}, f32[256,512]{1,0:T(8,128)S(1)}, u32[]{:S(2)}, u32[]{:S(2)}) collective-permute-start(f32[256,512]{1,0:T(8,128)S(1)} %collective-permute-done.4), channel_id=1, source_target_pairs={{0,8},{8,16},{16,24},{24,0},{1,9},{9,17},{17,25},{25,1},{2,10},{10... | collective-permute-start | bytes 1572872 | tf_op jit(solution)/shard_map/ppermute | solution.py:28
  425.4 11.9 %copy-start.2 = (f32[1024,1024]{1,0:T(8,128)S(1)}, f32[1024,1024]{1,0:T(8,128)}, u32[]{:S(2)}) copy-start(f32[1024,1024]{1,0:T(8,128)} %all-gather.9.cloned.1.call-done) | copy-start | bytes 12582916
  445.6 99.1 %copy-start.6 = (f32[256,128]{1,0:T(8,128)S(1)}, f32[256,128]{1,0:T(8,128)}, u32[]{:S(2)}) copy-start(f32[256,128]{1,0:T(8,128)} %subtract_divide_fusion.1) | copy-start | bytes 393220
  445.6 99.1 %reduce-scatter.11.cloned.1.call-start = ((), (), s32[]{:S(2)}) async-start(), calls=%async_computation.11 | async-start | bytes 1179648 | tf_op jit(solution)/shard_map/reduce_scatter | solution.py:43
Sparse Core Ops, SparseCore 0:
  53.3 39.3 all-gather.4
  94.3 21.5 all-gather.6
  118.0 74.6 all-gather.8
  212.3 29.3 reduce-scatter.4
  245.7 64.8 reduce-scatter.6
  357.6 38.7 all-gather.10
  445.8 30.1 reduce-scatter.8
  480.0 64.6 reduce-scatter.10
